TPU v7x, 256 devices: a whole 4x4x8 slice. The times are simulated.
256 devices in a mesh: gx: 16 (over z, x_lo), gz: 16 (over y, x_hi, core).
Axes of the slice: x: 4 (x_hi: 2, x_lo: 2; x = x_hi * 2 + x_lo), y: 4, z: 8, core: 2. Of those that a mesh axis runs over, the one named last changes fastest.
Arguments:
- velocity: float32 [3, 128, 512, 384], P(None, 'gx', 'gz'), may hold values from -6 to 6
- y_gap: float32 [385], replicated, may hold values from 0.2 to 2
Outputs:
- eddy_visc: float32 [128, 512, 384], P('gx', 'gz')
- lm_field: float32 [128, 512, 384], P('gx', 'gz')
- mm_field: float32 [128, 512, 384], P('gx', 'gz')
- coefficient: float32 [384], replicated
All inputs are finite; a program needn't handle non-finite values.
Results may differ from a plain program's by a relative error of at most 0.00002.
Values sent between devices are 32-bit elements; how exact they have to be, the bound alone decides.
No kernel may reach another device: no remote copies, remote signals or barrier semaphores. Data moves between devices by JAX's collectives and lax.ppermute only.
A program may use at most 64 MiB of HBM per device.

v0:
```python
import functools

import jax
import jax.numpy as jnp
from jax import lax
from jax.sharding import Mesh
from jax.sharding import PartitionSpec as P

GX_GZ = ("gx_0", "gx_1", "gz_0", "gz_1", "gz_2")
GX = ("gx_0", "gx_1")
GZ = ("gz_0", "gz_1", "gz_2")


WEIGHTS = (1.0, 1.0, 1.0, 2.0, 2.0, 2.0)


def extended(array, sides, width):
    for axis, dim in sides:
        size, length = (lax.axis_size(axis), array.shape[dim])
        up = [(i, (i + 1) % size) for i in range(size)]
        down = [(j, i) for i, j in up]
        last = lax.slice_in_dim(array, length - width, length, axis=dim)
        leading = lax.slice_in_dim(array, 0, width, axis=dim)
        before = lax.ppermute(last, axis, up)
        after = lax.ppermute(leading, axis, down)
        array = jnp.concatenate([before, array, after], axis=dim)
    return array


def over_axes(array, axes):
    return functools.reduce(lax.psum, axes, array)


def wall_slope(values, y_gap):
    padded = jnp.pad(values, [(0, 0)] * (values.ndim - 1) + [(1, 1)])
    return (padded[..., 2:] - padded[..., :-2]) / (y_gap[:-1] + y_gap[1:])


def strain_parts(slope_x, slope_y, slope_z):
    return jnp.stack(
        [
            slope_x[0],
            slope_y[1],
            slope_z[2],
            0.5 * (slope_y[0] + slope_x[1]),
            0.5 * (slope_z[0] + slope_x[2]),
            0.5 * (slope_z[1] + slope_y[2]),
        ]
    )


def contract(first_part, second_part):
    summed = first_part[0] * second_part[0]
    for component in range(1, 6):
        summed = summed + WEIGHTS[component] * first_part[component] * second_part[component]
    return summed


def magnitude(strain):
    return jnp.sqrt(2.0 * contract(strain, strain))


def pair_products(speeds):
    return jnp.stack(
        [
            speeds[0] * speeds[0],
            speeds[1] * speeds[1],
            speeds[2] * speeds[2],
            speeds[0] * speeds[1],
            speeds[0] * speeds[2],
            speeds[1] * speeds[2],
        ]
    )


def width_square(y_gap):
    return (0.5 * (y_gap[:-1] + y_gap[1:])) ** (2.0 / 3.0)


def germano(smooth_velocity, smooth_pairs, smooth_stress, test_strain, width_sq):
    leonard = smooth_pairs - pair_products(smooth_velocity)
    model_term = 2.0 * width_sq * (smooth_stress - 4.0 * magnitude(test_strain) * test_strain)
    return (contract(leonard, model_term), contract(model_term, model_term))


def rim_strain(padded, y_gap):
    slope_x = (padded[:, 2:, 1:-1] - padded[:, :-2, 1:-1]) * 0.5
    slope_z = (padded[:, 1:-1, 2:] - padded[:, 1:-1, :-2]) * 0.5
    slope_y = wall_slope(padded[:, 1:-1, 1:-1], y_gap)
    return strain_parts(slope_x, slope_y, slope_z)


def rim_filter(values):
    along_x = 0.25 * values[:, :-2] + 0.5 * values[:, 1:-1] + 0.25 * values[:, 2:]
    return 0.25 * along_x[:, :, :-2] + 0.5 * along_x[:, :, 1:-1] + 0.25 * along_x[:, :, 2:]


def per_device(velocity, y_gap):
    width_sq = width_square(y_gap)
    padded = extended(velocity, ((GX, 1), (GZ, 2)), 2)
    strain_wide = rim_strain(padded, y_gap)
    size_wide = magnitude(strain_wide)
    inner = padded[:, 1:-1, 1:-1]
    smooth_pairs = rim_filter(pair_products(inner))
    smooth_stress = rim_filter(size_wide * strain_wide)
    smooth_wide = rim_filter(padded)
    smooth_velocity = smooth_wide[:, 1:-1, 1:-1]
    test_strain = rim_strain(smooth_wide, y_gap)
    strain_size = size_wide[1:-1, 1:-1]
    lm_field, mm_field = germano(
        smooth_velocity, smooth_pairs, smooth_stress, test_strain, width_sq
    )
    planes = velocity.shape[1] * lax.axis_size(GX) * velocity.shape[2] * lax.axis_size(GZ)
    plane_pair = jnp.stack([jnp.sum(lm_field, axis=(0, 1)), jnp.sum(mm_field, axis=(0, 1))])
    total_pair = over_axes(plane_pair, GX_GZ)
    coefficient = total_pair[0] / planes / (total_pair[1] / planes + 1e-06)
    eddy_visc = coefficient * width_sq * strain_size
    return (eddy_visc, lm_field, mm_field, coefficient)


def solution(mesh):
    torus = Mesh(mesh.devices.reshape(8, 2, 4, 2, 2), ("gx_0", "gx_1", "gz_0", "gz_1", "gz_2"))
    return jax.shard_map(
        per_device,
        mesh=torus,
        in_specs=(P(None, GX, GZ, None), P()),
        out_specs=(P(GX, GZ, None), P(GX, GZ, None), P(GX, GZ, None), P()),
        check_vma=False,
    )
```

profile of v0, /device:TPU:1, one launch (start us, length us, event | category | flops | bytes accessed | tf_op | source)
XLA Modules:
  0.0 85.4 jit_solution(11277026666586406063)
XLA Ops:
  0.7 1.2 %fusion.70 = (f32[3,2,32,384]{3,2,1,0:T(8,128)S(1)}, f32[3,2,32,384]{3,2,1,0:T(8,128)S(1)}) fusion(f32[3,8,32,384]{3,2,1,0:T(8,128)} %param.2), kind=kLoop, calls=%fused_computation.159 | loop fusion | bytes 1179648 | tf_op jit(solution)/shard_map/slice | solution.py:23
  1.8 2.1 %collective-permute-start = (f32[3,2,32,384]{3,2,1,0:T(8,128)S(1)}, f32[3,2,32,384]{3,2,1,0:T(8,128)S(1)}, u32[]{:S(2)}, u32[]{:S(2)}) collective-permute-start(f32[3,2,32,384]{3,2,1,0:T(8,128)S(1)} %get-tuple-element.30), channel_id=1, source_target_pairs={{0,16},{16,32},{32,48},{48,64},{64,80},{80,96},{96,112},{112,128},... | collective-permute-start | bytes 884744 | tf_op jit(solution)/shard_map/ppermute | solution.py:24
  3.9 5.4 %collective-permute-start.1 = (f32[3,2,32,384]{3,2,1,0:T(8,128)S(1)}, f32[3,2,32,384]{3,2,1,0:T(8,128)S(1)}, u32[]{:S(2)}, u32[]{:S(2)}) collective-permute-start(f32[3,2,32,384]{3,2,1,0:T(8,128)S(1)} %get-tuple-element.29), channel_id=1, source_target_pairs={{16,0},{32,16},{48,32},{64,48},{80,64},{96,80},{112,96},{128,112},... | collective-permute-start | bytes 884744 | tf_op jit(solution)/shard_map/ppermute | solution.py:25
  9.3 6.7 %collective-permute-done = f32[3,2,32,384]{3,2,1,0:T(8,128)S(1)} collective-permute-done((f32[3,2,32,384]{3,2,1,0:T(8,128)S(1)}, f32[3,2,32,384]{3,2,1,0:T(8,128)S(1)}, u32[]{:S(2)}, u32[]{:S(2)}) %collective-permute-start) | collective-permute-done | bytes 294944 | tf_op jit(solution)/shard_map/ppermute | solution.py:24
  16.1 1.7 %collective-permute-done.1 = f32[3,2,32,384]{3,2,1,0:T(8,128)S(1)} collective-permute-done((f32[3,2,32,384]{3,2,1,0:T(8,128)S(1)}, f32[3,2,32,384]{3,2,1,0:T(8,128)S(1)}, u32[]{:S(2)}, u32[]{:S(2)}) %collective-permute-start.1) | collective-permute-done | bytes 294944 | tf_op jit(solution)/shard_map/ppermute | solution.py:25
  18.0 2.1 %collective-permute-start.3 = (f32[3,12,2,384]{3,2,1,0:T(2,128)S(1)}, f32[3,12,2,384]{3,2,1,0:T(2,128)S(1)}, u32[]{:S(2)}, u32[]{:S(2)}) collective-permute-start(f32[3,12,2,384]{3,2,1,0:T(2,128)S(1)} %get-tuple-element.28), channel_id=1, source_target_pairs={{1,0},{2,1},{3,2},{4,3},{5,4},{6,5},{7,6},{8,7},{9,8},{10,9},{11,1... | collective-permute-start | bytes 331784 | tf_op jit(solution)/shard_map/ppermute | solution.py:25
  20.0 2.9 %collective-permute-start.2 = (f32[3,12,2,384]{3,2,1,0:T(2,128)S(1)}, f32[3,12,2,384]{3,2,1,0:T(2,128)S(1)}, u32[]{:S(2)}, u32[]{:S(2)}) collective-permute-start(f32[3,12,2,384]{3,2,1,0:T(2,128)S(1)} %get-tuple-element.27), channel_id=1, source_target_pairs={{0,1},{1,2},{2,3},{3,4},{4,5},{5,6},{6,7},{7,8},{8,9},{9,10},{10,1... | collective-permute-start | bytes 331784 | tf_op jit(solution)/shard_map/ppermute | solution.py:24
  23.0 2.1 %collective-permute-done.3 = f32[3,12,2,384]{3,2,1,0:T(2,128)S(1)} collective-permute-done((f32[3,12,2,384]{3,2,1,0:T(2,128)S(1)}, f32[3,12,2,384]{3,2,1,0:T(2,128)S(1)}, u32[]{:S(2)}, u32[]{:S(2)}) %collective-permute-start.3) | collective-permute-done | bytes 110624 | tf_op jit(solution)/shard_map/ppermute | solution.py:25
  25.1 0.3 pad_maximum_fusion
  25.4 0.3 fusion.15
  25.7 0.3 fusion.18
  25.9 0.5 fusion.16
  26.5 0.4 fusion.22
  27.0 1.3 %fusion.12 = (f32[3,10,34,384]{3,2,1,0:T(8,128)S(1)}, f32[3,10,34,384]{3,2,1,0:T(8,128)S(1)}) fusion(f32[3,10,34,384]{3,2,1,0:T(8,128)S(1)} %get-tuple-element.22, f32[384]{0:T(512)S(1)} %get-tuple-element.9, f32[3,12,32,384]{3,2,1,0:T(8,128)S(1)} %constant_dynamic-update-slice_fusion, f32[3,12,2,384]{3,2,1,0:T(2,128)S(1)} %collective-permute-done.2, ...), kind=kLoop, calls=%fused_computation.27 | loop fusion | flops 2350080 | bytes 6692352 | tf_op jit(solution)/shard_map/div | solution.py:36
  28.3 0.6 fusion.29
  29.2 0.3 broadcast_multiply_fusion
  29.5 0.4 fusion
  29.9 0.7 fusion.21
  30.7 0.4 fusion.36
  31.7 0.1 multiply_dynamic-update-slice_fusion.5
  31.8 0.1 multiply_dynamic-update-slice_fusion.4
  31.9 0.1 multiply_dynamic-update-slice_fusion.3
  32.0 0.4 fusion.2
  32.4 0.9 %fusion.9 = f32[6,8,32,384]{3,2,1,0:T(8,128)S(1)} fusion(f32[6,8,32,384]{3,2,1,0:T(8,128)S(1)} %multiply_dynamic-update-slice_fusion.12, f32[6,8,34,384]{3,2,1,0:T(8,128)S(1)} %fusion.2), kind=kLoop, calls=%fused_computation.21 | loop fusion | flops 3538944 | bytes 11796480 | tf_op jit(solution)/shard_map/sub | solution.py:81
  33.3 0.9 %fusion.6 = f32[6,8,32,384]{3,2,1,0:T(8,128)S(1)} fusion(f32[6,8,34,384]{3,2,1,0:T(8,128)S(1)} %fusion, f32[6,8,32,384]{3,2,1,0:T(8,128)S(1)} %multiply_dynamic-update-slice_fusion.9, f32[8,32,384]{2,1,0:T(8,128)S(1)} %get-tuple-element.19, f32[384]{0:T(512)S(1)} %get-tuple-element.8), kind=kLoop, calls=%fused_computation.15 | loop fusion | flops 4718592 | bytes 12191232 | tf_op jit(solution)/shard_map/mul | solution.py:82
  34.2 1.4 %fusion.65 = (f32[384]{0:T(512)S(1)}, f32[8,32,384]{2,1,0:T(8,128)}, f32[384]{0:T(512)S(1)}, f32[8,32,384]{2,1,0:T(8,128)}) fusion(f32[6,8,32,384]{3,2,1,0:T(8,128)S(1)} %fusion.6, f32[6,8,32,384]{3,2,1,0:T(8,128)S(1)} %fusion.9), kind=kLoop, calls=%fused_computation.156 | loop fusion | flops 2948352 | bytes 5508096 | tf_op jit(solution)/shard_map/reduce_sum | solution.py:114
  35.7 16.8 %psum.35 = f32[2,384]{1,0:T(2,128)S(1)} all-reduce(f32[2,384]{1,0:T(2,128)S(1)} %pad_maximum_fusion.3), channel_id=1, replica_groups=mesh['gx_0'=8,'gx_1'=2,'gz_0'=4,'gz_1'=2,'gz_2'=2] {'gx_0'}, use_global_device_ids=true, to_apply=%region_2.3 | all-reduce | flops 768 | bytes 6144 | tf_op jit(solution)/shard_map/psum | solution.py:31
  52.4 3.8 %psum.36 = f32[2,384]{1,0:T(2,128)S(1)} all-reduce(f32[2,384]{1,0:T(2,128)S(1)} %psum.35), channel_id=1, replica_groups=mesh['gx_0'=8,'gx_1'=2,'gz_0'=4,'gz_1'=2,'gz_2'=2] {'gx_1'}, use_global_device_ids=true, to_apply=%region_3.4 | all-reduce | flops 768 | bytes 6144 | tf_op jit(solution)/shard_map/psum | solution.py:31
  56.2 8.3 %psum.37 = f32[2,384]{1,0:T(2,128)S(1)} all-reduce(f32[2,384]{1,0:T(2,128)S(1)} %psum.36), channel_id=1, replica_groups=mesh['gx_0'=8,'gx_1'=2,'gz_0'=4,'gz_1'=2,'gz_2'=2] {'gz_0'}, use_global_device_ids=true, to_apply=%region_4.5 | all-reduce | flops 768 | bytes 6144 | tf_op jit(solution)/shard_map/psum | solution.py:31
  64.5 6.7 %psum.38 = f32[2,384]{1,0:T(2,128)S(1)} all-reduce(f32[2,384]{1,0:T(2,128)S(1)} %psum.37), channel_id=1, replica_groups=mesh['gx_0'=8,'gx_1'=2,'gz_0'=4,'gz_1'=2,'gz_2'=2] {'gz_1'}, use_global_device_ids=true, to_apply=%region_5.6 | all-reduce | flops 768 | bytes 6144 | tf_op jit(solution)/shard_map/psum | solution.py:31
  71.2 13.0 %psum.39 = f32[2,384]{1,0:T(2,128)S(1)} all-reduce(f32[2,384]{1,0:T(2,128)S(1)} %psum.38), channel_id=1, replica_groups=mesh['gx_0'=8,'gx_1'=2,'gz_0'=4,'gz_1'=2,'gz_2'=2] {'gz_2'}, use_global_device_ids=true, to_apply=%region_6.7 | all-reduce | flops 768 | bytes 6144 | tf_op jit(solution)/shard_map/psum | solution.py:31
  84.3 1.1 %fusion.44 = f32[8,32,384]{2,1,0:T(8,128)} fusion(f32[10,34,384]{2,1,0:T(8,128)S(1)} %get-tuple-element.14, f32[10,34,384]{2,1,0:T(8,128)S(1)} %get-tuple-element.12, f32[10,34,384]{2,1,0:T(8,128)S(1)} %get-tuple-element.16, f32[10,34,384]{2,1,0:T(8,128)S(1)} %broadcast_multiply_fusion.1, f32[10,34,384]{2,1,0:T(8,128)S(1)} %bitcast.69, f32[384]{0:T(512)S(1)} %fusion.57), kind=kLoop, calls=%fused_computation.103 | loop fusion | flops 983040 | bytes 2360832 | tf_op jit(solution)/shard_map/mul | solution.py:117
  (37 shorter events, 1.5 us)
Async XLA Ops:
  0.6 15.4 %copy-start = (f32[3,8,32,384]{3,2,1,0:T(8,128)S(1)}, f32[3,8,32,384]{3,2,1,0:T(8,128)}, u32[]{:S(2)}) copy-start(f32[3,8,32,384]{3,2,1,0:T(8,128)} %param.2) | copy-start | bytes 3538948
  0.6 22.3 %copy-start.2 = (f32[385]{0:T(512)S(1)}, f32[385]{0:T(512)}, u32[]{:S(2)}) copy-start(f32[385]{0:T(512)} %param.3) | copy-start | bytes 4624
  1.8 14.2 %collective-permute-start = (f32[3,2,32,384]{3,2,1,0:T(8,128)S(1)}, f32[3,2,32,384]{3,2,1,0:T(8,128)S(1)}, u32[]{:S(2)}, u32[]{:S(2)}) collective-permute-start(f32[3,2,32,384]{3,2,1,0:T(8,128)S(1)} %get-tuple-element.30), channel_id=1, source_target_pairs={{0,16},{16,32},{32,48},{48,64},{64,80},{80,96},{96,112},{112,128},... | collective-permute-start | bytes 884744 | tf_op jit(solution)/shard_map/ppermute | solution.py:24
  3.9 13.9 %collective-permute-start.1 = (f32[3,2,32,384]{3,2,1,0:T(8,128)S(1)}, f32[3,2,32,384]{3,2,1,0:T(8,128)S(1)}, u32[]{:S(2)}, u32[]{:S(2)}) collective-permute-start(f32[3,2,32,384]{3,2,1,0:T(8,128)S(1)} %get-tuple-element.29), channel_id=1, source_target_pairs={{16,0},{32,16},{48,32},{64,48},{80,64},{96,80},{112,96},{128,112},... | collective-permute-start | bytes 884744 | tf_op jit(solution)/shard_map/ppermute | solution.py:25
  18.0 7.1 %collective-permute-start.3 = (f32[3,12,2,384]{3,2,1,0:T(2,128)S(1)}, f32[3,12,2,384]{3,2,1,0:T(2,128)S(1)}, u32[]{:S(2)}, u32[]{:S(2)}) collective-permute-start(f32[3,12,2,384]{3,2,1,0:T(2,128)S(1)} %get-tuple-element.28), channel_id=1, source_target_pairs={{1,0},{2,1},{3,2},{4,3},{5,4},{6,5},{7,6},{8,7},{9,8},{10,9},{11,1... | collective-permute-start | bytes 331784 | tf_op jit(solution)/shard_map/ppermute | solution.py:25
  20.0 5.1 %collective-permute-start.2 = (f32[3,12,2,384]{3,2,1,0:T(2,128)S(1)}, f32[3,12,2,384]{3,2,1,0:T(2,128)S(1)}, u32[]{:S(2)}, u32[]{:S(2)}) collective-permute-start(f32[3,12,2,384]{3,2,1,0:T(2,128)S(1)} %get-tuple-element.27), channel_id=1, source_target_pairs={{0,1},{1,2},{2,3},{3,4},{4,5},{5,6},{6,7},{7,8},{8,9},{9,10},{10,1... | collective-permute-start | bytes 331784 | tf_op jit(solution)/shard_map/ppermute | solution.py:24
  84.2 1.2 %copy-start.1 = (f32[384]{0:T(512)}, f32[384]{0:T(512)S(1)}, u32[]{:S(2)}) copy-start(f32[384]{0:T(512)S(1)} %fusion.61) | copy-start | bytes 4612
where the time goes:
time: 85.6 us; the launch traced here: 85.4 us
  blocking collectives  48.5 us (57%)
  starting transfers between devices  12.4 us (14%)
  other arithmetic  11.4 us (13%)
  waiting for transfers between devices  10.5 us (12%)
  local copies, waits for them, and re-layouts  1.59 us (2%)
  between operations  0.96 us (1%)
    psum x5, blocking collectives, over_axes(): return functools.reduce(lax.psum, axes, array)  48.5 us
    ppermute x2, starting transfers between devices, extended(): after = lax.ppermute(leading, axis, down)  7.43 us
    ppermute x2, waiting for transfers between devices, extended(): before = lax.ppermute(last, axis, up)  6.67 us
    ppermute x2, starting transfers between devices, extended(): before = lax.ppermute(last, axis, up)  5.01 us
    ppermute x2, waiting for transfers between devices, extended(): after = lax.ppermute(leading, axis, down)  3.8 us
    div x2, other arithmetic, wall_slope(): return (padded[..., 2:] - padded[..., :-2]) / (y_gap[:-1] + y_gap[1:])  1.94 us
  transfers between devices with their start and end apart: 4, of which 3 were waited for; matrix products, arithmetic and copies ran while one was open for 0% of the time, Pallas kernels for 0%

commit v1 on v0

--- a/solution.py
+++ b/solution.py
@@ -6,7 +6,6 @@
 from jax.sharding import Mesh
 from jax.sharding import PartitionSpec as P
 
-GX_GZ = ("gx_0", "gx_1", "gz_0", "gz_1", "gz_2")
 GX = ("gx_0", "gx_1")
 GZ = ("gz_0", "gz_1", "gz_2")
 
@@ -27,8 +26,16 @@
     return array
 
 
-def over_axes(array, axes):
-    return functools.reduce(lax.psum, axes, array)
+def over_group(array, axes):
+    members = functools.reduce(lambda count, axis: count * lax.axis_size(axis), axes, 1)
+    copies = jnp.broadcast_to(array[None], (members, *array.shape))
+    return jnp.sum(lax.all_to_all(copies, axes, 0, 0, tiled=True), axis=0)
+
+
+def over_axes(array):
+    for axes in (("gx_0", "gz_2"), ("gx_1", "gz_0", "gz_1")):
+        array = over_group(array, axes)
+    return array
 
 
 def wall_slope(values, y_gap):
@@ -112,7 +119,7 @@
     )
     planes = velocity.shape[1] * lax.axis_size(GX) * velocity.shape[2] * lax.axis_size(GZ)
     plane_pair = jnp.stack([jnp.sum(lm_field, axis=(0, 1)), jnp.sum(mm_field, axis=(0, 1))])
-    total_pair = over_axes(plane_pair, GX_GZ)
+    total_pair = over_axes(plane_pair)
     coefficient = total_pair[0] / planes / (total_pair[1] / planes + 1e-06)
     eddy_visc = coefficient * width_sq * strain_size
     return (eddy_visc, lm_field, mm_field, coefficient)

time: 85.6 us -> 70.4 us (0.82)
  blocking collectives: 48.5 us -> 22.7 us
  waiting for transfers between devices: 10.5 us -> 16.9 us
  starting transfers between devices: 12.4 us -> 15.9 us
    psum x5 -> x0, blocking collectives: 48.5 us -> none  [over_axes(): return functools.reduce(lax.psum, axes, array)]
    all_to_all x0 -> x1, blocking collectives: none -> 22.7 us  [over_group(): return jnp.sum(lax.all_to_all(copies, axes, 0, 0, tiled=True), axis=0)]
    all_to_all x0 -> x1, waiting for transfers between devices: none -> 6.48 us  [over_group(): return jnp.sum(lax.all_to_all(copies, axes, 0, 0, tiled=True), axis=0)]
    all_to_all x0 -> x1, starting transfers between devices: none -> 3.5 us  [over_group(): return jnp.sum(lax.all_to_all(copies, axes, 0, 0, tiled=True), axis=0)]
  transfers between devices with their start and end apart: 4 -> 5, of which waited for: 3 -> 4; matrix products, arithmetic and copies ran while one was open for 0% -> 0% of each run, Pallas kernels for 0% -> 0%
where the time goes in v1:
time: 70.4 us; the launch traced here: 70.2 us
  blocking collectives  22.7 us (32%)
  waiting for transfers between devices  16.9 us (24%)
  starting transfers between devices  15.9 us (23%)
  other arithmetic  11.5 us (16%)
  local copies, waits for them, and re-layouts  2.24 us (3%)
  between operations  0.97 us (1%)
    all_to_all x1, blocking collectives, over_group(): return jnp.sum(lax.all_to_all(copies, axes, 0, 0, tiled=True), axis=0)  22.7 us
    ppermute x2, starting transfers between devices, extended(): after = lax.ppermute(leading, axis, down)  7.43 us
    ppermute x2, waiting for transfers between devices, extended(): before = lax.ppermute(last, axis, up)  6.67 us
    all_to_all x1, waiting for transfers between devices, over_group(): return jnp.sum(lax.all_to_all(copies, axes, 0, 0, tiled=True), axis=0)  6.48 us
    ppermute x2, starting transfers between devices, extended(): before = lax.ppermute(last, axis, up)  5.01 us
    ppermute x2, waiting for transfers between devices, extended(): after = lax.ppermute(leading, axis, down)  3.8 us
    all_to_all x1, starting transfers between devices, over_group(): return jnp.sum(lax.all_to_all(copies, axes, 0, 0, tiled=True), axis=0)  3.5 us
    div x2, other arithmetic, wall_slope(): return (padded[..., 2:] - padded[..., :-2]) / (y_gap[:-1] + y_gap[1:])  1.94 us
  transfers between devices with their start and end apart: 5, of which 4 were waited for; matrix products, arithmetic and copies ran while one was open for 0% of the time, Pallas kernels for 0%

profile of v1, /device:TPU:1, one launch (start us, length us, event | category | flops | bytes accessed | tf_op | source)
XLA Modules:
  0.0 70.2 jit_solution(4599261363407620199)
XLA Ops:
  0.7 1.2 %fusion.70 = (f32[3,2,32,384]{3,2,1,0:T(8,128)S(1)}, f32[3,2,32,384]{3,2,1,0:T(8,128)S(1)}) fusion(f32[3,8,32,384]{3,2,1,0:T(8,128)} %param.2), kind=kLoop, calls=%fused_computation.159 | loop fusion | bytes 1179648 | tf_op jit(solution)/shard_map/slice | solution.py:22
  1.8 2.1 %collective-permute-start = (f32[3,2,32,384]{3,2,1,0:T(8,128)S(1)}, f32[3,2,32,384]{3,2,1,0:T(8,128)S(1)}, u32[]{:S(2)}, u32[]{:S(2)}) collective-permute-start(f32[3,2,32,384]{3,2,1,0:T(8,128)S(1)} %get-tuple-element.30), channel_id=1, source_target_pairs={{0,16},{16,32},{32,48},{48,64},{64,80},{80,96},{96,112},{112,128},... | collective-permute-start | bytes 884744 | tf_op jit(solution)/shard_map/ppermute | solution.py:23
  3.9 5.4 %collective-permute-start.1 = (f32[3,2,32,384]{3,2,1,0:T(8,128)S(1)}, f32[3,2,32,384]{3,2,1,0:T(8,128)S(1)}, u32[]{:S(2)}, u32[]{:S(2)}) collective-permute-start(f32[3,2,32,384]{3,2,1,0:T(8,128)S(1)} %get-tuple-element.29), channel_id=1, source_target_pairs={{16,0},{32,16},{48,32},{64,48},{80,64},{96,80},{112,96},{128,112},... | collective-permute-start | bytes 884744 | tf_op jit(solution)/shard_map/ppermute | solution.py:24
  9.3 6.7 %collective-permute-done = f32[3,2,32,384]{3,2,1,0:T(8,128)S(1)} collective-permute-done((f32[3,2,32,384]{3,2,1,0:T(8,128)S(1)}, f32[3,2,32,384]{3,2,1,0:T(8,128)S(1)}, u32[]{:S(2)}, u32[]{:S(2)}) %collective-permute-start) | collective-permute-done | bytes 294944 | tf_op jit(solution)/shard_map/ppermute | solution.py:23
  16.1 1.7 %collective-permute-done.1 = f32[3,2,32,384]{3,2,1,0:T(8,128)S(1)} collective-permute-done((f32[3,2,32,384]{3,2,1,0:T(8,128)S(1)}, f32[3,2,32,384]{3,2,1,0:T(8,128)S(1)}, u32[]{:S(2)}, u32[]{:S(2)}) %collective-permute-start.1) | collective-permute-done | bytes 294944 | tf_op jit(solution)/shard_map/ppermute | solution.py:24
  18.0 2.1 %collective-permute-start.3 = (f32[3,12,2,384]{3,2,1,0:T(2,128)S(1)}, f32[3,12,2,384]{3,2,1,0:T(2,128)S(1)}, u32[]{:S(2)}, u32[]{:S(2)}) collective-permute-start(f32[3,12,2,384]{3,2,1,0:T(2,128)S(1)} %get-tuple-element.28), channel_id=1, source_target_pairs={{1,0},{2,1},{3,2},{4,3},{5,4},{6,5},{7,6},{8,7},{9,8},{10,9},{11,1... | collective-permute-start | bytes 331784 | tf_op jit(solution)/shard_map/ppermute | solution.py:24
  20.0 2.9 %collective-permute-start.2 = (f32[3,12,2,384]{3,2,1,0:T(2,128)S(1)}, f32[3,12,2,384]{3,2,1,0:T(2,128)S(1)}, u32[]{:S(2)}, u32[]{:S(2)}) collective-permute-start(f32[3,12,2,384]{3,2,1,0:T(2,128)S(1)} %get-tuple-element.27), channel_id=1, source_target_pairs={{0,1},{1,2},{2,3},{3,4},{4,5},{5,6},{6,7},{7,8},{8,9},{9,10},{10,1... | collective-permute-start | bytes 331784 | tf_op jit(solution)/shard_map/ppermute | solution.py:23
  23.0 2.1 %collective-permute-done.3 = f32[3,12,2,384]{3,2,1,0:T(2,128)S(1)} collective-permute-done((f32[3,12,2,384]{3,2,1,0:T(2,128)S(1)}, f32[3,12,2,384]{3,2,1,0:T(2,128)S(1)}, u32[]{:S(2)}, u32[]{:S(2)}) %collective-permute-start.3) | collective-permute-done | bytes 110624 | tf_op jit(solution)/shard_map/ppermute | solution.py:24
  25.1 0.3 pad_maximum_fusion
  25.4 0.3 fusion.15
  25.7 0.3 fusion.18
  25.9 0.5 fusion.16
  26.5 0.4 fusion.22
  27.0 1.3 %fusion.12 = (f32[3,10,34,384]{3,2,1,0:T(8,128)S(1)}, f32[3,10,34,384]{3,2,1,0:T(8,128)S(1)}) fusion(f32[3,10,34,384]{3,2,1,0:T(8,128)S(1)} %get-tuple-element.22, f32[384]{0:T(512)S(1)} %get-tuple-element.9, f32[3,12,32,384]{3,2,1,0:T(8,128)S(1)} %constant_dynamic-update-slice_fusion, f32[3,12,2,384]{3,2,1,0:T(2,128)S(1)} %collective-permute-done.2, ...), kind=kLoop, calls=%fused_computation.27 | loop fusion | flops 2350080 | bytes 6692352 | tf_op jit(solution)/shard_map/div | solution.py:43
  28.3 0.6 fusion.29
  29.1 0.1 multiply_dynamic-update-slice_fusion
  29.2 0.3 broadcast_multiply_fusion
  29.5 0.4 fusion
  29.9 0.7 fusion.21
  30.7 0.4 fusion.36
  31.6 0.1 multiply_dynamic-update-slice_fusion.5
  31.8 0.1 multiply_dynamic-update-slice_fusion.4
  31.9 0.1 multiply_dynamic-update-slice_fusion.3
  32.0 0.4 fusion.2
  32.4 0.9 %fusion.9 = f32[6,8,32,384]{3,2,1,0:T(8,128)S(1)} fusion(f32[6,8,32,384]{3,2,1,0:T(8,128)S(1)} %multiply_dynamic-update-slice_fusion.12, f32[6,8,34,384]{3,2,1,0:T(8,128)S(1)} %fusion.2), kind=kLoop, calls=%fused_computation.21 | loop fusion | flops 3538944 | bytes 11796480 | tf_op jit(solution)/shard_map/sub | solution.py:88
  33.3 0.9 %fusion.6 = f32[6,8,32,384]{3,2,1,0:T(8,128)S(1)} fusion(f32[6,8,34,384]{3,2,1,0:T(8,128)S(1)} %fusion, f32[6,8,32,384]{3,2,1,0:T(8,128)S(1)} %multiply_dynamic-update-slice_fusion.9, f32[8,32,384]{2,1,0:T(8,128)S(1)} %get-tuple-element.19, f32[384]{0:T(512)S(1)} %get-tuple-element.8), kind=kLoop, calls=%fused_computation.15 | loop fusion | flops 4718592 | bytes 12191232 | tf_op jit(solution)/shard_map/mul | solution.py:89
  34.2 1.4 %fusion.65 = (f32[384]{0:T(512)S(1)}, f32[8,32,384]{2,1,0:T(8,128)}, f32[384]{0:T(512)S(1)}, f32[8,32,384]{2,1,0:T(8,128)}) fusion(f32[6,8,32,384]{3,2,1,0:T(8,128)S(1)} %fusion.6, f32[6,8,32,384]{3,2,1,0:T(8,128)S(1)} %fusion.9), kind=kLoop, calls=%fused_computation.156 | loop fusion | flops 2948352 | bytes 5508096 | tf_op jit(solution)/shard_map/reduce_sum | solution.py:121
  35.7 22.7 %all_to_all.10 = f32[16,2,384]{2,1,0:T(2,128)S(1)} all-to-all(f32[16,2,384]{2,1,0:T(2,128)S(1)} %broadcast_in_dim.4), channel_id=1, replica_groups=mesh['gx_0'=8,'gx_1'=2,'gz_0'=4,'gz_1'=2,'gz_2'=2] {'gx_0','gz_2'}, dimensions={0} | all-to-all | bytes 98304 | tf_op jit(solution)/shard_map/all_to_all | solution.py:32
  58.4 0.6 broadcast_in_dim.5
  59.0 3.5 %all-to-all-start.1 = ((f32[16,2,384]{2,1,0:T(2,128)}), f32[16,2,384]{2,1,0:T(2,128)S(1)}, u32[]{:S(2)}, u32[]{:S(2)}) async-start(f32[16,2,384]{2,1,0:T(2,128)} %broadcast_in_dim.5), calls=%async_computation.1 | async-start | bytes 98304 | tf_op jit(solution)/shard_map/all_to_all | solution.py:32
  62.5 6.5 %all-to-all-done.1 = f32[16,2,384]{2,1,0:T(2,128)S(1)} async-done(((f32[16,2,384]{2,1,0:T(2,128)}), f32[16,2,384]{2,1,0:T(2,128)S(1)}, u32[]{:S(2)}, u32[]{:S(2)}) %all-to-all-start.1) | async-done | bytes 49184 | tf_op jit(solution)/shard_map/all_to_all | solution.py:32
  69.1 1.1 %fusion.44 = f32[8,32,384]{2,1,0:T(8,128)} fusion(f32[10,34,384]{2,1,0:T(8,128)S(1)} %get-tuple-element.14, f32[10,34,384]{2,1,0:T(8,128)S(1)} %get-tuple-element.12, f32[10,34,384]{2,1,0:T(8,128)S(1)} %get-tuple-element.16, f32[10,34,384]{2,1,0:T(8,128)S(1)} %broadcast_multiply_fusion.1, f32[10,34,384]{2,1,0:T(8,128)S(1)} %bitcast.69, f32[384]{0:T(512)S(1)} %fusion.57), kind=kLoop, calls=%fused_computation.103 | loop fusion | flops 983040 | bytes 2360832 | tf_op jit(solution)/shard_map/mul | solution.py:124
  (39 shorter events, 1.4 us)
Async XLA Ops:
  0.6 15.4 %copy-start = (f32[3,8,32,384]{3,2,1,0:T(8,128)S(1)}, f32[3,8,32,384]{3,2,1,0:T(8,128)}, u32[]{:S(2)}) copy-start(f32[3,8,32,384]{3,2,1,0:T(8,128)} %param.2) | copy-start | bytes 3538948
  0.6 22.3 %copy-start.2 = (f32[385]{0:T(512)S(1)}, f32[385]{0:T(512)}, u32[]{:S(2)}) copy-start(f32[385]{0:T(512)} %param.3) | copy-start | bytes 4624
  1.8 14.2 %collective-permute-start = (f32[3,2,32,384]{3,2,1,0:T(8,128)S(1)}, f32[3,2,32,384]{3,2,1,0:T(8,128)S(1)}, u32[]{:S(2)}, u32[]{:S(2)}) collective-permute-start(f32[3,2,32,384]{3,2,1,0:T(8,128)S(1)} %get-tuple-element.30), channel_id=1, source_target_pairs={{0,16},{16,32},{32,48},{48,64},{64,80},{80,96},{96,112},{112,128},... | collective-permute-start | bytes 884744 | tf_op jit(solution)/shard_map/ppermute | solution.py:23
  3.9 13.9 %collective-permute-start.1 = (f32[3,2,32,384]{3,2,1,0:T(8,128)S(1)}, f32[3,2,32,384]{3,2,1,0:T(8,128)S(1)}, u32[]{:S(2)}, u32[]{:S(2)}) collective-permute-start(f32[3,2,32,384]{3,2,1,0:T(8,128)S(1)} %get-tuple-element.29), channel_id=1, source_target_pairs={{16,0},{32,16},{48,32},{64,48},{80,64},{96,80},{112,96},{128,112},... | collective-permute-start | bytes 884744 | tf_op jit(solution)/shard_map/ppermute | solution.py:24
  18.0 7.1 %collective-permute-start.3 = (f32[3,12,2,384]{3,2,1,0:T(2,128)S(1)}, f32[3,12,2,384]{3,2,1,0:T(2,128)S(1)}, u32[]{:S(2)}, u32[]{:S(2)}) collective-permute-start(f32[3,12,2,384]{3,2,1,0:T(2,128)S(1)} %get-tuple-element.28), channel_id=1, source_target_pairs={{1,0},{2,1},{3,2},{4,3},{5,4},{6,5},{7,6},{8,7},{9,8},{10,9},{11,1... | collective-permute-start | bytes 331784 | tf_op jit(solution)/shard_map/ppermute | solution.py:24
  20.0 5.1 %collective-permute-start.2 = (f32[3,12,2,384]{3,2,1,0:T(2,128)S(1)}, f32[3,12,2,384]{3,2,1,0:T(2,128)S(1)}, u32[]{:S(2)}, u32[]{:S(2)}) collective-permute-start(f32[3,12,2,384]{3,2,1,0:T(2,128)S(1)} %get-tuple-element.27), channel_id=1, source_target_pairs={{0,1},{1,2},{2,3},{3,4},{4,5},{5,6},{6,7},{7,8},{8,9},{9,10},{10,1... | collective-permute-start | bytes 331784 | tf_op jit(solution)/shard_map/ppermute | solution.py:23
  59.0 10.0 %all-to-all-start.1 = ((f32[16,2,384]{2,1,0:T(2,128)}), f32[16,2,384]{2,1,0:T(2,128)S(1)}, u32[]{:S(2)}, u32[]{:S(2)}) async-start(f32[16,2,384]{2,1,0:T(2,128)} %broadcast_in_dim.5), calls=%async_computation.1 | async-start | bytes 98304 | tf_op jit(solution)/shard_map/all_to_all | solution.py:32
  69.1 1.1 %copy-start.1 = (f32[384]{0:T(512)}, f32[384]{0:T(512)S(1)}, u32[]{:S(2)}) copy-start(f32[384]{0:T(512)S(1)} %fusion.61) | copy-start | bytes 4612
